TPU v7x, 8 devices: a whole 2x2x1 slice. The times are simulated.
8 devices in a mesh: dp: 1 (over z), tp: 8 (over y, x, core).
Axes of the slice: x: 2, y: 2, z: 1, core: 2. Of those that a mesh axis runs over, the one named last changes fastest.
Arguments:
- x_in: bfloat16 [8, 2048, 2560], P('dp', 'tp')
- ln_gain: float32 [2, 2560], replicated
- ln_bias: float32 [2, 2560], replicated
- w_qkv: bfloat16 [2, 2560, 3, 32, 80], P(None, None, None, 'tp')
- w_out: bfloat16 [2, 32, 80, 2560], P(None, 'tp')
- b_out: float32 [2, 2560], replicated
- w_up: bfloat16 [2, 2560, 10240], P(None, None, 'tp')
- b_up: float32 [2, 10240], P(None, 'tp')
- w_down: bfloat16 [2, 10240, 2560], P(None, 'tp')
- b_down: float32 [2, 2560], replicated
Outputs:
- output: bfloat16 [8, 2048, 2560], P('dp', 'tp')
All inputs are finite; a program needn't handle non-finite values.
Results may differ from a plain program's by a relative error of at most 0.0128346.
Values are sent between devices in bfloat16 or wider.
A program may use at most 1 GiB of HBM per device.

v0:
```python
import jax
import jax.numpy as jnp
from jax import lax
from jax.sharding import PartitionSpec as P

LN_EPS = 1e-5


def layer_norm(residual, gain, bias):
    row_mean = jnp.mean(residual, axis=-1, keepdims=True)
    centered = residual - row_mean
    row_var = jnp.mean(centered * centered, axis=-1, keepdims=True)
    return (centered * lax.rsqrt(row_var + LN_EPS) * gain + bias).astype(jnp.bfloat16)


def query_block(batch, heads, q_len, k_len):
    block = q_len
    while block % 2 == 0 and block > 16 and batch * heads * block * k_len > 2 ** 24:
        block = block // 2
    return block


def causal_attention(queries, keys, values, q_start):
    batch, q_len, heads, head_dim = queries.shape
    k_len = keys.shape[1]
    block = query_block(batch, heads, q_len, k_len)
    inv_sqrt = head_dim ** -0.5
    key_pos = jnp.arange(k_len)

    def one_block(index):
        q_blk = lax.dynamic_slice_in_dim(queries, index * block, block, axis=1)
        scores = jnp.einsum('bqhe,bkhe->bhqk', q_blk, keys, preferred_element_type=jnp.float32) * inv_sqrt
        q_pos = q_start + index * block + jnp.arange(block)
        scores = jnp.where(key_pos[None, :] <= q_pos[:, None], scores, -jnp.inf)
        attn_prob = jax.nn.softmax(scores, axis=-1).astype(jnp.bfloat16)
        return jnp.einsum('bhqk,bkhe->bqhe', attn_prob, values, preferred_element_type=jnp.float32).astype(jnp.bfloat16)

    out_blocks = lax.map(one_block, jnp.arange(q_len // block))
    return jnp.moveaxis(out_blocks, 0, 1).reshape(batch, q_len, heads, head_dim)


def solution(mesh):
    tp_size = mesh.shape['tp']
    act_spec = P('dp', 'tp', None)

    def layer(residual, ln_gain, ln_bias, w_qkv, w_out, w_up, bias_up, w_down, bias_sum):
        normed = layer_norm(residual, ln_gain, ln_bias)
        gathered = lax.all_gather(normed, 'tp', axis=1, tiled=True)
        qkv_all = jnp.einsum('bsd,dthe->bsthe', gathered, w_qkv, preferred_element_type=jnp.float32).astype(jnp.bfloat16)
        attn_out = causal_attention(qkv_all[:, :, 0], qkv_all[:, :, 1], qkv_all[:, :, 2], 0)
        partial = jnp.einsum('bshe,hed->bsd', attn_out, w_out, preferred_element_type=jnp.float32)
        hidden = jnp.einsum('bsd,df->bsf', gathered, w_up, preferred_element_type=jnp.float32) + bias_up
        gelu_out = jax.nn.gelu(hidden, approximate=True).astype(jnp.bfloat16)
        partial = partial + jnp.einsum('bsf,fd->bsd', gelu_out, w_down, preferred_element_type=jnp.float32)
        received = lax.all_to_all(partial.astype(jnp.bfloat16), 'tp', 1, 1, tiled=True)
        batch, seq_len, width = received.shape
        summed = jnp.sum(received.reshape(batch, tp_size, seq_len // tp_size, width), axis=1, dtype=jnp.float32)
        return residual + (summed + bias_sum)

    def local_fn(x_in, ln_gain, ln_bias, w_qkv, w_out, b_out, w_up, b_up, w_down, b_down):
        residual = x_in.astype(jnp.float32)
        for layer_idx in range(w_qkv.shape[0]):
            residual = layer(residual, ln_gain[layer_idx], ln_bias[layer_idx], w_qkv[layer_idx], w_out[layer_idx],
                             w_up[layer_idx], b_up[layer_idx], w_down[layer_idx], b_out[layer_idx] + b_down[layer_idx])
        return residual.astype(jnp.bfloat16)

    in_specs = (act_spec, P(), P(), P(None, None, None, 'tp', None), P(None, 'tp', None, None), P(),
                P(None, None, 'tp'), P(None, 'tp'), P(None, 'tp', None), P())
    return jax.shard_map(local_fn, mesh=mesh, in_specs=in_specs, out_specs=act_spec, check_vma=False)
```

profile of v0, /device:TPU:0, one launch (start us, length us, event | category | flops | bytes accessed | tf_op | source)
XLA Modules:
  0.0 4815.9 jit_solution(10932048943997286511)
XLA Ops:
  6.5 5.6 convert_reduce_fusion.2
  12.1 7.0 fusion.76
  19.9 7.3 fusion.79
  27.8 370.7 %all-gather.3.cloned.1.call-done = bf16[8,2048,2560]{2,1,0:T(8,128)(2,1)} async-done(((bf16[8,256,2560]{2,1,0:T(8,128)(2,1)}), bf16[8,2048,2560]{2,1,0:T(8,128)(2,1)}) %all-gather.3.cloned.1.call-update) | async-done | bytes 83886096 | tf_op jit(solution)/shard_map/all_gather | solution.py:48
  398.5 90.0 %fusion.82 = bf16[8,2048,3,4,80]{1,4,3,2,0:T(8,128)(2,1)} fusion(bf16[8,2048,2560]{2,1,0:T(8,128)(2,1)} %all-gather.3.cloned.1.call-done, bf16[2,2560,3,4,80]{1,4,3,2,0:T(8,128)(2,1)} %param.17), kind=kOutput, calls=%fused_computation.89 | convolution fusion | flops 80546365440 | bytes 120258560 | tf_op jit(solution)/shard_map/bsd,dthe->bsthe/dot_general | solution.py:49
  488.6 23.5 slice_bitcast_fusion.3
  512.1 5.4 broadcast.77.clone
  517.5 483.1 %while.22 = (s32[]{:T(128)}, bf16[8,8,256,4,80]{2,4,3,1,0:T(8,128)(2,1)}, s32[8]{0:T(128)S(1)}, bf16[8,2048,4,80]{1,3,2,0:T(8,128)(2,1)}, bf16[8,2048,4,80]{1,3,...) while((s32[]{:T(128)}, ...), condition=%wide.region_5.6_spmd.clone, body=%wide.region_2.5_spmd.clone.sunk | while | flops 5470554112 | bytes 158927024 | solution.py:38
  519.4 31.4 fusion.188
  550.7 27.3 fusion.189
  579.7 31.3 fusion.188
  611.1 27.3 fusion.189
  640.1 31.3 fusion.188
  671.4 27.3 fusion.189
  700.5 31.3 fusion.188
  731.8 27.3 fusion.189
  760.8 31.3 fusion.188
  792.2 27.3 fusion.189
  821.2 31.3 fusion.188
  852.5 27.3 fusion.189
  881.5 31.3 fusion.188
  912.9 27.3 fusion.189
  941.9 31.3 fusion.188
  973.3 27.3 fusion.189
  1000.5 9.6 copy.27
  1010.1 62.7 %fusion.106 = f32[8,2048,2560,1]{2,1,3,0:T(8,128)} fusion(bf16[8,2048,4,80]{1,3,2,0:T(8,128)(2,1)} %bitcast.168, bf16[2,4,80,2560]{3,2,1,0:T(8,128)(2,1)S(1)} %copy-done.13), kind=kOutput, calls=%fused_computation.111 | convolution fusion | flops 26843545600 | bytes 179896320 | tf_op jit(solution)/shard_map/bshe,hed->bsd/dot_general | solution.py:51
  1072.8 138.9 %fusion.61.clone.5 = bf16[8,2048,1280]{2,1,0:T(8,128)(2,1)} fusion(bf16[8,2048,2560]{2,1,0:T(8,128)(2,1)} %all-gather.3.cloned.1.call-done, f32[1280]{0:T(1024)S(1)} %copy-done.12, bf16[2,2560,1280]{2,1,0:T(8,128)(2,1)} %param.20), kind=kOutput, calls=%fused_computation.61.clone.clone.clone.2 | convolution fusion | flops 107583897600 | bytes 132387840 | tf_op jit(solution)/shard_map/bsd,df->bsf/dot_general | solution.py:52
  1211.8 120.4 %fusion.53 = bf16[8,2048,2560]{2,1,0:T(8,128)(2,1)} fusion(f32[8,2048,2560,1]{2,1,3,0:T(8,128)} %fusion.106, bf16[2,1280,2560]{2,1,0:T(8,128)(2,1)} %param.22, bf16[8,2048,1280]{2,1,0:T(8,128)(2,1)} %fusion.61.clone.5), kind=kOutput, calls=%fused_computation.51 | convolution fusion | flops 107458068480 | bytes 300154880 | tf_op jit(solution)/shard_map/bsf,fd->bsd/dot_general | solution.py:54
  1332.2 74.1 %copy.18 = bf16[8,2048,2560]{2,0,1:T(8,128)(2,1)} copy(bf16[8,2048,2560]{2,1,0:T(8,128)(2,1)} %fusion.53) | data formatting | bytes 167772160 | tf_op jit(solution)/shard_map/convert_element_type | solution.py:55
  1406.3 10.2 all-to-all-start
  1417.2 903.0 %all-to-all-done = bf16[8,2048,2560]{2,0,1:T(8,128)(2,1)} async-done(((bf16[8,2048,2560]{2,0,1:T(8,128)(2,1)}), bf16[8,2048,2560]{2,0,1:T(8,128)(2,1)}, u32[]{:S(2)}, u32[]{:S(2)}) %all-to-all-start) | async-done | bytes 83886112 | tf_op jit(solution)/shard_map/all_to_all | solution.py:55
  2320.2 44.5 convert_reduce_fusion.1
  2364.8 19.2 fusion.118
  2384.0 16.3 multiply_reduce_fusion
  2400.3 26.9 add_convert_fusion
  2427.3 368.2 %all-gather.5.cloned.1.call-done = bf16[8,2048,2560]{2,1,0:T(8,128)(2,1)} async-done(((bf16[8,256,2560]{2,1,0:T(8,128)(2,1)}), bf16[8,2048,2560]{2,1,0:T(8,128)(2,1)}) %all-gather.5.cloned.1.call-update) | async-done | bytes 83886096 | tf_op jit(solution)/shard_map/all_gather | solution.py:48
  2795.5 90.4 %fusion.85 = bf16[8,2048,3,4,80]{1,4,3,2,0:T(8,128)(2,1)} fusion(bf16[8,2048,2560]{2,1,0:T(8,128)(2,1)} %all-gather.5.cloned.1.call-done, bf16[2,2560,3,4,80]{1,4,3,2,0:T(8,128)(2,1)} %param.17), kind=kOutput, calls=%fused_computation.90 | convolution fusion | flops 80546365440 | bytes 120258560 | tf_op jit(solution)/shard_map/bsd,dthe->bsthe/dot_general | solution.py:49
  2886.0 23.5 slice_bitcast_fusion
  2909.4 5.4 broadcast.77
  2914.8 481.7 %while.23 = (s32[]{:T(128)}, bf16[8,8,256,4,80]{2,4,3,1,0:T(8,128)(2,1)}, s32[8]{0:T(128)S(1)}, bf16[8,2048,4,80]{1,3,2,0:T(8,128)(2,1)}, bf16[8,2048,4,80]{1,3,...) while((s32[]{:T(128)}, ...), condition=%wide.region_12.13_spmd.clone, body=%wide.region_9.12_spmd.clone.sunk | while | flops 5470554112 | bytes 158927024 | solution.py:38
  2916.5 31.4 fusion.193
  2947.9 27.2 fusion.194
  2976.7 31.4 fusion.193
  3008.1 27.2 fusion.194
  3036.9 31.4 fusion.193
  3068.3 27.2 fusion.194
  3097.1 31.4 fusion.193
  3128.5 27.2 fusion.194
  3157.3 31.4 fusion.193
  3188.7 27.2 fusion.194
  3217.5 31.4 fusion.193
  3248.8 27.2 fusion.194
  3277.7 31.4 fusion.193
  3309.0 27.2 fusion.194
  3337.9 31.4 fusion.193
  3369.2 27.2 fusion.194
  3396.4 9.6 copy.28
  3406.0 62.7 %fusion.104 = f32[8,2048,2560,1]{2,1,3,0:T(8,128)} fusion(bf16[8,2048,4,80]{1,3,2,0:T(8,128)(2,1)} %bitcast.169, bf16[2,4,80,2560]{3,2,1,0:T(8,128)(2,1)S(1)} %copy-done.14), kind=kOutput, calls=%fused_computation.109 | convolution fusion | flops 26843545600 | bytes 179896320 | tf_op jit(solution)/shard_map/bshe,hed->bsd/dot_general | solution.py:51
  3468.7 138.9 %fusion.69.clone.5 = bf16[8,2048,1280]{2,1,0:T(8,128)(2,1)} fusion(bf16[8,2048,2560]{2,1,0:T(8,128)(2,1)} %all-gather.5.cloned.1.call-done, f32[1280]{0:T(1024)S(1)} %copy-done.11, bf16[2,2560,1280]{2,1,0:T(8,128)(2,1)} %param.20), kind=kOutput, calls=%fused_computation.69.clone.clone.clone.2 | convolution fusion | flops 107583897600 | bytes 132387840 | tf_op jit(solution)/shard_map/bsd,df->bsf/dot_general | solution.py:52
  3607.7 120.5 %fusion.52 = bf16[8,2048,2560]{2,1,0:T(8,128)(2,1)} fusion(f32[8,2048,2560,1]{2,1,3,0:T(8,128)} %fusion.104, bf16[2,1280,2560]{2,1,0:T(8,128)(2,1)} %param.22, bf16[8,2048,1280]{2,1,0:T(8,128)(2,1)} %fusion.69.clone.5), kind=kOutput, calls=%fused_computation.49 | convolution fusion | flops 107458068480 | bytes 300154880 | tf_op jit(solution)/shard_map/bsf,fd->bsd/dot_general | solution.py:54
  3728.1 74.1 %copy.21 = bf16[8,2048,2560]{2,0,1:T(8,128)(2,1)} copy(bf16[8,2048,2560]{2,1,0:T(8,128)(2,1)} %fusion.52) | data formatting | bytes 167772160 | tf_op jit(solution)/shard_map/convert_element_type | solution.py:55
  3802.3 926.1 %all_to_all.10 = bf16[8,2048,2560]{2,0,1:T(8,128)(2,1)} all-to-all(bf16[8,2048,2560]{2,0,1:T(8,128)(2,1)} %copy.21), channel_id=1, replica_groups=mesh['dp'=1,'tp'=8] {'tp'}, dimensions={1} | all-to-all | bytes 167772160 | tf_op jit(solution)/shard_map/all_to_all | solution.py:55
  4728.3 51.1 %convert_reduce_fusion = f32[8,256,2560]{2,0,1:T(8,128)} fusion(bf16[8,8,256,2560]{3,0,2,1:T(8,128)(2,1)} %bitcast.43), kind=kLoop, calls=%fused_computation.46 | loop fusion | flops 78643200 | bytes 104857600 | tf_op jit(solution)/shard_map/reduce_sum | solution.py:57
  4779.5 29.4 fusion.81
  (116 shorter events, 18.0 us)
Async XLA Ops:
  6.5 12.6 copy-start.8
  6.5 12.6 copy-start.9
  6.5 392.0 %all-gather.3.cloned.1.call-start = ((), (), s32[]{:S(2)}) async-start(), calls=%async_computation.2 | async-start | bytes 94371840 | tf_op jit(solution)/shard_map/all_gather | solution.py:48
  6.5 13.3 slice-start.5
  6.5 13.3 slice-start.6
  12.1 7.7 slice-start.7
  12.1 15.1 copy-start.10
  1000.5 9.6 copy-start.13
  1010.1 62.7 %copy-start.12 = (f32[1280]{0:T(1024)S(1)}, f32[1280]{0:T(1024)}, u32[]{:S(2)}) copy-start(f32[1280]{0:T(1024)} %get-tuple-element.116) | copy-start | bytes 15364
  1406.3 10.2 copy-start.6
  1406.3 10.3 copy-start.7
  1406.3 913.9 %all-to-all-start = ((bf16[8,2048,2560]{2,0,1:T(8,128)(2,1)}), bf16[8,2048,2560]{2,0,1:T(8,128)(2,1)}, u32[]{:S(2)}, u32[]{:S(2)}) async-start(bf16[8,2048,2560]{2,0,1:T(8,128)(2,1)} %copy.18), calls=%async_computation | async-start | bytes 167772160 | tf_op jit(solution)/shard_map/all_to_all | solution.py:55
  1416.5 1379.0 %all-gather.5.cloned.1.call-start = ((), (), s32[]{:S(2)}) async-start(), calls=%async_computation.3 | async-start | bytes 94371840 | tf_op jit(solution)/shard_map/all_gather | solution.py:48
  1417.2 983.1 %copy-start.1 = (f32[2560]{0:T(1024)}, f32[2560]{0:T(1024)S(1)}, u32[]{:S(2)}) copy-start(f32[2560]{0:T(1024)S(1)} %get-tuple-element.110) | copy-start | bytes 30724
  2364.7 35.6 copy-start
  2364.7 19.2 slice-start.8
  2364.7 19.2 slice-start.9
  2364.7 19.2 slice-start.10
  2383.9 16.4 copy-start.4
  2383.9 16.4 copy-start.5
  3396.4 9.6 copy-start.14
  3406.0 62.7 %copy-start.11 = (f32[1280]{0:T(1024)S(1)}, f32[1280]{0:T(1024)}, u32[]{:S(2)}) copy-start(f32[1280]{0:T(1024)} %get-tuple-element.115) | copy-start | bytes 15364
  3802.2 977.2 %slice-start = ((s8[20971520]{0:T(1024)(128)(4,1)}), s8[4194304]{0:T(1024)(128)(4,1)S(1)}, s32[]{:S(2)}) async-start(s8[20971520]{0:T(1024)(128)(4,1)} %bitcast.160), calls=%async_computation.4 | async-start | bytes 8388608
  3802.3 977.2 %slice-start.1 = ((s8[20971520]{0:T(1024)(128)(4,1)}), s8[4194304]{0:T(1024)(128)(4,1)S(1)}, s32[]{:S(2)}) async-start(s8[20971520]{0:T(1024)(128)(4,1)} %bitcast.160), calls=%async_computation.5 | async-start | bytes 8388608
  3802.3 977.2 %slice-start.2 = ((s8[20971520]{0:T(1024)(128)(4,1)}), s8[4194304]{0:T(1024)(128)(4,1)S(1)}, s32[]{:S(2)}) async-start(s8[20971520]{0:T(1024)(128)(4,1)} %bitcast.160), calls=%async_computation.6 | async-start | bytes 8388608
  3802.3 977.1 %slice-start.3 = ((s8[20971520]{0:T(1024)(128)(4,1)}), s8[4194304]{0:T(1024)(128)(4,1)S(1)}, s32[]{:S(2)}) async-start(s8[20971520]{0:T(1024)(128)(4,1)} %bitcast.160), calls=%async_computation.7 | async-start | bytes 8388608
  4728.3 51.1 %slice-start.4 = ((s8[20971520]{0:T(1024)(128)(4,1)}), s8[4194304]{0:T(1024)(128)(4,1)S(1)}, s32[]{:S(2)}) async-start(s8[20971520]{0:T(1024)(128)(4,1)} %bitcast.160), calls=%async_computation.8 | async-start | bytes 8388608
  4728.3 51.1 %copy-start.2 = (f32[2560]{0:T(1024)S(1)}, f32[2560]{0:T(1024)}, u32[]{:S(2)}) copy-start(f32[2560]{0:T(1024)} %copy-done.1) | copy-start | bytes 30724
  4728.3 51.1 %copy-start.3 = (f32[2560]{0:T(1024)S(1)}, f32[2560]{0:T(1024)}, u32[]{:S(2)}) copy-start(f32[2560]{0:T(1024)} %get-tuple-element.109) | copy-start | bytes 30724
Sparse Core Ops, SparseCore 0:
  27.3 371.1 all-gather.2
  2427.4 368.0 all-gather.4
where the time goes:
time: 4820 us
  matrix products  1760 us (37%)
  waiting for transfers between devices  1640 us (34%)
  blocking collectives  926 us (19%)
  local copies, waits for them, and re-layouts  237 us (5%)
  other arithmetic  214 us (4%)
    all_to_all x1, blocking collectives, layer(): lax.all_to_all(partial.astype(jnp.bfloat16), 'tp', 1, 1, tiled=True)  926 us
    all_to_all x1, waiting for transfers between devices, layer(): lax.all_to_all(partial.astype(jnp.bfloat16), 'tp', 1, 1, tiled=True)  903 us
    all_gather x2, waiting for transfers between devices, layer(): gathered = lax.all_gather(normed, 'tp', axis=1, tiled=True)  739 us
    sub x16, matrix products, one_block(): attn_prob = jax.nn.softmax(scores, axis=-1).astype(jnp.bfloat16)  502 us
    dot_general x16, matrix products, one_block(): jnp.einsum('bhqk,bkhe->bqhe', attn_prob, values, preferred_element_type=j...  436 us
    dot_general x2, matrix products, layer(): jnp.einsum('bsd,df->bsf', gathered, w_up, preferred_element_type=jnp.floa...  278 us
    dot_general x2, matrix products, layer(): jnp.einsum('bsf,fd->bsd', gelu_out, w_down, preferred_element_type=jnp.fl...  241 us
    dot_general x2, matrix products, layer(): jnp.einsum('bsd,dthe->bsthe', gathered, w_qkv, preferred_element_type=jnp...  180 us
  transfers between devices with their start and end apart: 3, of which 3 were waited for; matrix products, arithmetic and copies ran while one was open for 0% of the time, Pallas kernels for 0%

commit v1 on v0

v1 whole, which is shorter than its diff:
```python
import functools

import jax
import jax.numpy as jnp
from jax import lax
from jax.experimental import pallas as pl
from jax.experimental.pallas import tpu as pltpu
from jax.sharding import PartitionSpec as P


LN_EPS = 1e-5
LOG2_E = 1.4426950408889634
BLK = 256
SHARDS = 4
VMEM_LIMIT = 62 * 2 ** 20


def attn_kernel(pos_ref, *refs, heads, dim):
    own, oth = refs[:SHARDS], refs[SHARDS:2 * SHARDS]
    o_own, o_oth, q_s, k_s, v_s, o_s, s_a, s_b, p_a, p_b = refs[2 * SHARDS:]
    tokens = o_s.shape[1]
    per_half = o_own.shape[0] // BLK
    for half, group in enumerate((own, oth)):
        for rel in range(per_half):
            off = pl.multiple_of(pos_ref[half * per_half + rel], BLK)
            cols = slice(rel * BLK, (rel + 1) * BLK)
            for shard, ref in enumerate(group):
                def stage(h, _, ref=ref, shard=shard, cols=cols, off=off):
                    def rows(t):
                        return pl.ds(pl.multiple_of((t * heads + h) * dim, 16), dim)

                    head = shard * heads + h
                    q_s[head, :, pl.ds(off, BLK)] = ref[rows(0), cols]
                    k_s[head, pl.ds(off, BLK), :dim] = ref[rows(1), cols].T
                    v_s[head, :, pl.ds(off, BLK)] = ref[rows(2), cols]
                    return 0

                lax.fori_loop(0, heads, stage, 0, unroll=True)

    scale = dim ** -0.5 * LOG2_E
    n_q = tokens // BLK
    s_bufs, p_bufs = (s_a, s_b), (p_a, p_b)

    def one_head(head, _):
        keep = (lax.broadcasted_iota(jnp.int32, (BLK, BLK), 0)
                <= lax.broadcasted_iota(jnp.int32, (BLK, BLK), 1))

        def scores(qi):
            end = (qi + 1) * BLK
            s_ref = s_bufs[qi % 2]
            s = jnp.dot(k_s[head, :end, :dim], q_s[head, :, qi * BLK:end], preferred_element_type=jnp.float32)
            if qi:
                s_ref[:end - BLK, :] = s[:end - BLK]
            s_ref[end - BLK:end, :] = jnp.where(keep, s[end - BLK:], -jnp.inf)

        def soften(qi):
            s_ref, p_ref = s_bufs[qi % 2], p_bufs[qi % 2]
            top = None
            for ki in range(qi + 1):
                cur = s_ref[ki * BLK:(ki + 1) * BLK, :].reshape(BLK // 8, 8, BLK).max(axis=0)
                top = cur if top is None else jnp.maximum(top, cur)
            top = top.max(axis=0, keepdims=True) * scale
            total = None
            for ki in range(qi + 1):
                p = jnp.exp2(s_ref[ki * BLK:(ki + 1) * BLK, :] * scale - top)
                part = p.reshape(BLK // 8, 8, BLK).sum(axis=0)
                total = part if total is None else total + part
                p_ref[ki * BLK:(ki + 1) * BLK, :] = p.astype(jnp.bfloat16)
            return total.sum(axis=0, keepdims=True)

        def weigh(qi, total):
            end = (qi + 1) * BLK
            acc = jnp.dot(v_s[head, :, :end], p_bufs[qi % 2][:end, :], preferred_element_type=jnp.float32)
            rows = pl.ds(pl.multiple_of(head * dim, 16), dim)
            o_s[rows, qi * BLK:end] = (acc / total).astype(jnp.bfloat16)

        scores(0)
        previous = None
        for qi in range(n_q):
            if qi + 1 < n_q:
                scores(qi + 1)
            total = soften(qi)
            if previous is not None:
                weigh(qi - 1, previous)
            previous = total
        weigh(n_q - 1, previous)
        return 0

    lax.fori_loop(0, SHARDS * heads, one_head, 0)
    for half, out in enumerate((o_own, o_oth)):
        for rel in range(per_half):
            off = pl.multiple_of(pos_ref[half * per_half + rel], BLK)
            out[rel * BLK:(rel + 1) * BLK, :] = o_s[:, pl.ds(off, BLK)].T


def attention(pos, own, oth, heads, dim):
    half_tokens = own[0].shape[1]
    tokens, all_heads = 2 * half_tokens, SHARDS * heads
    shape = jax.ShapeDtypeStruct((half_tokens, all_heads * dim), jnp.bfloat16)
    vmem = pl.BlockSpec(memory_space=pltpu.VMEM)
    return pl.pallas_call(
        functools.partial(attn_kernel, heads=heads, dim=dim),
        out_shape=(shape, shape),
        in_specs=[pl.BlockSpec(memory_space=pltpu.SMEM)] + [vmem] * (2 * SHARDS),
        out_specs=(vmem, vmem),
        scratch_shapes=[
            pltpu.VMEM((all_heads, dim, tokens), jnp.bfloat16),
            pltpu.VMEM((all_heads, tokens, 128), jnp.bfloat16),
            pltpu.VMEM((all_heads, dim, tokens), jnp.bfloat16),
            pltpu.VMEM((all_heads * dim, tokens), jnp.bfloat16),
            pltpu.VMEM((tokens, BLK), jnp.float32),
            pltpu.VMEM((tokens, BLK), jnp.float32),
            pltpu.VMEM((tokens, BLK), jnp.bfloat16),
            pltpu.VMEM((tokens, BLK), jnp.bfloat16),
        ],
        compiler_params=pltpu.CompilerParams(vmem_limit_bytes=VMEM_LIMIT),
        cost_estimate=pl.CostEstimate(
            flops=5 * all_heads * tokens * tokens * dim, bytes_accessed=4 * 2 * tokens * all_heads * dim,
            transcendentals=all_heads * tokens * tokens // 2),
    )(pos, *own, *oth)


def combine_kernel(*refs, first):
    n = (len(refs) - 3) // 2
    lhs_hbm, rhs, (out, lhs, sems) = refs[:n], refs[n:2 * n], refs[2 * n:]
    rows = out.shape[0]
    step = 512
    copies = [pltpu.make_async_copy(lhs_hbm[i].at[pl.ds(first, rows)], lhs.at[i], sems.at[i]) for i in range(n)]

    @pl.when(pl.program_id(0) == 0)
    def _():
        for copy in copies:
            copy.start()

    def product(wait):
        for r in range(0, rows, step):
            acc = None
            for i in range(n):
                if wait and r == 0:
                    copies[i].wait()
                term = jnp.dot(lhs[i, r:r + step, :], rhs[i][...], preferred_element_type=jnp.float32)
                acc = term if acc is None else acc + term
            out[r:r + step, :] = acc.astype(out.dtype)

    @pl.when(pl.program_id(0) == 0)
    def _():
        product(True)

    @pl.when(pl.program_id(0) > 0)
    def _():
        product(False)


def combine(lhs, rhs, dtype, first=0, rows=None):
    rows = rows or lhs[0].shape[0]
    depth = lhs[0].shape[1]
    width = rhs[0].shape[1]
    tile = 256
    return pl.pallas_call(
        functools.partial(combine_kernel, first=first),
        out_shape=jax.ShapeDtypeStruct((rows, width), dtype),
        grid=(width // tile,),
        in_specs=[pl.BlockSpec(memory_space=pl.ANY) for _ in lhs]
        + [pl.BlockSpec((depth, tile), lambda n: (0, n)) for _ in rhs],
        out_specs=pl.BlockSpec((rows, tile), lambda n: (0, n)),
        scratch_shapes=[pltpu.VMEM((len(lhs), rows, depth), jnp.bfloat16), pltpu.SemaphoreType.DMA((len(lhs),))],
        compiler_params=pltpu.CompilerParams(vmem_limit_bytes=VMEM_LIMIT, dimension_semantics=("arbitrary",)),
        cost_estimate=pl.CostEstimate(
            flops=2 * rows * depth * len(lhs) * width, bytes_accessed=2 * depth * len(lhs) * (rows + width) + 4 * rows * width,
            transcendentals=0),
    )(*lhs, *rhs)


def qkv_kernel(h_ref, w_a, w_b, out_a, out_b):
    step = pl.program_id(0)
    last = pl.num_programs(0) // 2

    def project(w_ref, out):
        h = h_ref[...]
        prod = lax.dot_general(w_ref[...], h, (((1,), (1,)), ((), ())), preferred_element_type=jnp.float32)
        out[...] = prod.astype(jnp.bfloat16)

    @pl.when(step < last)
    def _():
        project(w_a, out_a)

    @pl.when(step >= last)
    def _():
        project(w_b, out_b)


def qkv_pair(h, w_a, w_b):
    tokens, width = h.shape
    rows = w_a.shape[0]
    tile = rows // 2
    shape = jax.ShapeDtypeStruct((rows, tokens), jnp.bfloat16)
    early = lambda n: (jnp.minimum(n, 1), 0)
    late = lambda n: (jnp.maximum(n - 2, 0), 0)
    return pl.pallas_call(
        qkv_kernel,
        out_shape=(shape, shape),
        grid=(4,),
        in_specs=[pl.BlockSpec((tokens, width), lambda n: (0, 0), pipeline_mode=pl.Buffered(1)),
                  pl.BlockSpec((tile, width), early), pl.BlockSpec((tile, width), late)],
        out_specs=(pl.BlockSpec((tile, tokens), early), pl.BlockSpec((tile, tokens), late)),
        compiler_params=pltpu.CompilerParams(vmem_limit_bytes=VMEM_LIMIT, dimension_semantics=("arbitrary",)),
        cost_estimate=pl.CostEstimate(flops=4 * tokens * width * rows, bytes_accessed=2 * (tokens * width + 2 * rows * (width + tokens)),
                                      transcendentals=0),
    )(h, w_a, w_b)


def up_kernel(h_ref, *refs):
    n = len(refs) // 3
    weights, biases, outs = refs[:n], refs[n:2 * n], refs[2 * n:]
    per_shard = pl.num_programs(0) // n
    rows = h_ref.shape[0]
    for i in range(n):
        @pl.when(pl.program_id(0) // per_shard == i)
        def _(i=i):
            for r in range(0, rows, 512):
                hidden = jnp.dot(h_ref[r:r + 512, :], weights[i][...], preferred_element_type=jnp.float32) + biases[i][...]
                outs[i][r:r + 512, :] = jax.nn.gelu(hidden, approximate=True).astype(jnp.bfloat16)


def up(h, weights, biases):
    tokens, width = h.shape
    n, cols = len(weights), weights[0].shape[1]
    tile = 256
    per_shard = cols // tile
    at = [lambda s, i=i: (0, jnp.clip(s - i * per_shard, 0, per_shard - 1)) for i in range(n)]
    return pl.pallas_call(
        up_kernel,
        out_shape=[jax.ShapeDtypeStruct((tokens, cols), jnp.bfloat16)] * n,
        grid=(n * per_shard,),
        in_specs=[pl.BlockSpec((tokens, width), lambda s: (0, 0), pipeline_mode=pl.Buffered(1))]
        + [pl.BlockSpec((width, tile), m) for m in at] + [pl.BlockSpec((1, tile), m) for m in at],
        out_specs=[pl.BlockSpec((tokens, tile), m) for m in at],
        compiler_params=pltpu.CompilerParams(vmem_limit_bytes=VMEM_LIMIT, dimension_semantics=("arbitrary",)),
        cost_estimate=pl.CostEstimate(flops=2 * n * tokens * width * cols,
                                      bytes_accessed=2 * (tokens * width + n * cols * (width + tokens)),
                                      transcendentals=n * tokens * cols),
    )(h, *weights, *[b.reshape(1, cols) for b in biases])


def norm_block(res, gain, bias):
    mean = jnp.mean(res, axis=-1, keepdims=True)
    centered = res - mean
    var = jnp.mean(centered * centered, axis=-1, keepdims=True)
    return (centered * lax.rsqrt(var + LN_EPS) * gain + bias).astype(jnp.bfloat16)


def update_kernel(res, kept, received, bias_sum, gain, bias, res_out, h_out):
    new = res[...].astype(jnp.float32) + (kept[...] + received[...].astype(jnp.float32) + bias_sum[...])
    res_out[...] = new
    h_out[...] = norm_block(new, gain[...], bias[...])


def update_norm(res, kept, received, bias_sum, gain, bias):
    tokens, width = res.shape
    tile = 128
    row = pl.BlockSpec((tile, width), lambda n: (n, 0))
    vec = pl.BlockSpec((1, width), lambda n: (0, 0))
    return pl.pallas_call(
        update_kernel,
        out_shape=(jax.ShapeDtypeStruct((tokens, width), jnp.float32), jax.ShapeDtypeStruct((tokens, width), jnp.bfloat16)),
        grid=(tokens // tile,),
        in_specs=[row, row, row, vec, vec, vec],
        out_specs=(row, row),
        compiler_params=pltpu.CompilerParams(vmem_limit_bytes=VMEM_LIMIT, dimension_semantics=("arbitrary",)),
        cost_estimate=pl.CostEstimate(flops=10 * tokens * width, bytes_accessed=16 * tokens * width, transcendentals=0),
    )(res, kept, received, bias_sum.reshape(1, width), gain.reshape(1, width), bias.reshape(1, width))


def finish_kernel(res, kept, received, bias_sum, out):
    out[...] = (res[...] + (kept[...] + received[...].astype(jnp.float32) + bias_sum[...])).astype(jnp.bfloat16)


def finish(res, kept, received, bias_sum, first=0):
    tokens, width = kept.shape
    tile = 128
    row = pl.BlockSpec((tile, width), lambda n: (n, 0))
    res_row = pl.BlockSpec((tile, width), lambda n: (n + first // tile, 0))
    vec = pl.BlockSpec((1, width), lambda n: (0, 0))
    return pl.pallas_call(
        finish_kernel,
        out_shape=jax.ShapeDtypeStruct((tokens, width), jnp.bfloat16),
        grid=(tokens // tile,),
        in_specs=[res_row, row, row, vec],
        out_specs=row,
        compiler_params=pltpu.CompilerParams(vmem_limit_bytes=VMEM_LIMIT, dimension_semantics=("arbitrary",)),
        cost_estimate=pl.CostEstimate(flops=4 * tokens * width, bytes_accessed=12 * tokens * width, transcendentals=0),
    )(res, kept, received, bias_sum.reshape(1, width))


def first_kernel(res, gain, bias, h_out):
    h_out[...] = norm_block(res[...].astype(jnp.float32), gain[...], bias[...])


def first_norm(res, gain, bias):
    tokens, width = res.shape
    tile = 128
    row = pl.BlockSpec((tile, width), lambda n: (n, 0))
    vec = pl.BlockSpec((1, width), lambda n: (0, 0))
    return pl.pallas_call(
        first_kernel,
        out_shape=jax.ShapeDtypeStruct((tokens, width), jnp.bfloat16),
        grid=(tokens // tile,),
        in_specs=[row, vec, vec],
        out_specs=row,
        compiler_params=pltpu.CompilerParams(vmem_limit_bytes=VMEM_LIMIT, dimension_semantics=("arbitrary",)),
        cost_estimate=pl.CostEstimate(flops=10 * tokens * width, bytes_accessed=4 * tokens * width, transcendentals=0),
    )(res, gain.reshape(1, width), bias.reshape(1, width))


def solution(mesh):
    tp_size = mesh.shape['tp']
    act_spec = P('dp', 'tp', None)

    def swap(arr, mask):
        return lax.ppermute(arr, 'tp', [(i, i ^ mask) for i in range(tp_size)])

    SIB, XN, YN = 1, 2, 4
    HOPS = (0, SIB, YN, YN | SIB)

    def spread(shard):
        sibling = swap(shard, SIB)
        over_y = swap(shard, YN)
        diagonal = swap(over_y, SIB)
        return [shard, sibling, over_y, diagonal]

    def program(x_in, ln_gain, ln_bias, w_qkv, w_out, b_out, w_up, b_up, w_down, b_down):
        idx = lax.axis_index('tp')
        y, x, core = idx // 4, (idx // 2) % 2, idx % 2
        mine = y * 2 + core
        n_layers, width, _, heads, dim = w_qkv.shape
        batch, blk, _ = x_in.shape
        n_seq = batch // 4
        pos = jnp.stack([(((y ^ dy) * 2 + (x ^ dx)) * 2 + (core ^ dc)) * blk
                         for dx in (0, 1) for dy in (0, 1) for dc in (0, 1)]).astype(jnp.int32)

        by_group = x_in.reshape(4, n_seq, blk, width)
        parts = [[lax.dynamic_index_in_dim(by_group[:, k], mine ^ j, 0, keepdims=False) for j in range(4)]
                 for k in range(n_seq)]
        parts, w_qkv, w_up, w_down, w_out = lax.optimization_barrier((parts, w_qkv, w_up, w_down, w_out))
        residual = []
        for k in range(n_seq):
            pieces = []
            for j, mask in enumerate(HOPS):
                pieces.append(swap(parts[k][j], mask) if mask else parts[k][j])
            residual.append(jnp.concatenate(pieces, axis=0))

        b_up_all = spread(b_up)
        weights = []
        for l in range(n_layers):
            qkv_t = jnp.transpose(w_qkv[l], (1, 2, 3, 0)).reshape(3 * heads * dim, width)
            up_l, down_l, out_l = w_up[l], w_down[l], w_out[l].reshape(heads * dim, width)
            weights.append((spread(qkv_t), spread(up_l), spread(down_l),
                            jnp.concatenate(spread(out_l), axis=0)))

        h_own, finals = [], []
        for k in range(n_seq):
            h_own.append(first_norm(residual[k], ln_gain[0], ln_bias[0]))
        for l in range(n_layers):
            qkv_w, up_w, down_w, out_w = weights[l]
            bias_sum = b_out[l] + b_down[l]
            biases = [b[l] for b in b_up_all]
            for k in range(n_seq):
                h_other = swap(h_own[k], XN)
                qkv, gelu = [], []
                for h in (h_own[k], h_other):
                    qkv.append([])
                    gelu.append([])
                    for at in (0, 2):
                        qkv[-1] += qkv_pair(h, *qkv_w[at:at + 2])
                        if l == 0:
                            gelu[-1] += up(h, up_w[at:at + 2], biases[at:at + 2])
                    if l:
                        gelu[-1] += up(h, up_w, biases)
                o_own, o_oth = attention(pos, qkv[0], qkv[1], heads, dim)
                lhs_own, lhs_oth, rhs = [o_own] + gelu[0], [o_oth] + gelu[1], [out_w] + down_w
                if (l, k) == (n_layers - 1, n_seq - 1):
                    half = h_own[k].shape[0] // 2
                    ends = []
                    for first in (half, 0):
                        sent = combine(lhs_oth, rhs, jnp.bfloat16, first, half)
                        kept = combine(lhs_own, rhs, jnp.float32, first, half)
                        received = swap(sent, XN)
                        ends.append(finish(residual[k], kept, received, bias_sum, first))
                    finals.append(ends[1:] + ends[:1])
                    continue
                sent = combine(lhs_oth, rhs, jnp.bfloat16)
                kept = combine(lhs_own, rhs, jnp.float32)
                received = swap(sent, XN)
                if l + 1 < n_layers:
                    residual[k], h_own[k] = update_norm(residual[k], kept, received, bias_sum,
                                                        ln_gain[l + 1], ln_bias[l + 1])
                else:
                    finals.append([finish(residual[k], kept, received, bias_sum)])

        out = jnp.zeros((4, n_seq, blk, width), jnp.bfloat16)
        for k in range(n_seq):
            blocks = [f[at:at + blk] for f in finals[k] for at in range(0, f.shape[0], blk)]
            for j, mask in enumerate(HOPS):
                piece = blocks[j]
                piece = swap(piece, mask) if mask else piece
                out = lax.dynamic_update_slice(out, piece[None, None], (mine ^ j, k, 0, 0))
        return out.reshape(batch, blk, width)

    in_specs = (act_spec, P(), P(), P(None, None, None, 'tp', None), P(None, 'tp', None, None), P(),
                P(None, None, 'tp'), P(None, 'tp'), P(None, 'tp', None), P())
    return jax.shard_map(program, mesh=mesh, in_specs=in_specs, out_specs=act_spec, check_vma=False)
```

time: 4820 us -> 1980 us (0.41)
  matrix products: 1760 us -> 0 us
  Pallas kernels: 0 us -> 1320 us
  waiting for transfers between devices: 1640 us -> 532 us
  blocking collectives: 926 us -> 0 us
  other arithmetic: 214 us -> 12.4 us
  local copies, waits for them, and re-layouts: 237 us -> 84.2 us
    pallas_call x0 -> x49, Pallas kernels: none -> 1320 us  [the longest x10 371 us: combine(): pl.pallas_call(functools.partial(combine_kernel, first=first), out_shape=...]
    dot_general x24 -> x0, matrix products: 1260 us -> none  [the longest x16 436 us: one_block(): jnp.einsum('bhqk,bkhe->bqhe', attn_prob, values, preferred_element_type=j...]
    all_to_all x1 -> x0, blocking collectives: 926 us -> none  [layer(): lax.all_to_all(partial.astype(jnp.bfloat16), 'tp', 1, 1, tiled=True)]
    all_to_all x1 -> x0, waiting for transfers between devices: 903 us -> none  [layer(): lax.all_to_all(partial.astype(jnp.bfloat16), 'tp', 1, 1, tiled=True)]
    all_gather x2 -> x0, waiting for transfers between devices: 739 us -> none  [layer(): gathered = lax.all_gather(normed, 'tp', axis=1, tiled=True)]
    ppermute x0 -> x48, waiting for transfers between devices: none -> 532 us  [swap(): return lax.ppermute(arr, 'tp', [(i, i ^ mask) for i in range(tp_size)])]
    sub x16 -> x0, matrix products: 502 us -> none  [one_block(): attn_prob = jax.nn.softmax(scores, axis=-1).astype(jnp.bfloat16)]
    convert_element_type x2 -> x0, local copies, waits for them, and re-layouts: 148 us -> none  [layer(): partial.astype(jnp.bfloat16)]
  transfers between devices with their start and end apart: 3 -> 48, of which waited for: 3 -> 13; matrix products, arithmetic and copies ran while one was open for 0% -> 4% of each run, Pallas kernels for 0% -> 66%
where the time goes in v1:
time: 1980 us
  Pallas kernels  1320 us (67%)
  waiting for transfers between devices  532 us (27%)
  local copies, waits for them, and re-layouts  84.2 us (4%)
  starting transfers between devices  30.6 us (2%)
    ppermute x48, waiting for transfers between devices, swap(): return lax.ppermute(arr, 'tp', [(i, i ^ mask) for i in range(tp_size)])  532 us
    pallas_call x10, Pallas kernels, combine(): pl.pallas_call(functools.partial(combine_kernel, first=first), out_shape=...  371 us
    pallas_call x12, Pallas kernels, up(): pl.pallas_call(up_kernel, out_shape=[jax.ShapeDtypeStruct((tokens, cols),...  358 us
    pallas_call x16, Pallas kernels, qkv_pair(): pl.pallas_call(qkv_kernel, out_shape=(shape, shape), grid=(4,), in_specs=...  263 us
    pallas_call x4, Pallas kernels, attention(): pl.pallas_call(functools.partial(attn_kernel, heads=heads, dim=dim), out_...  252 us
  transfers between devices with their start and end apart: 48, of which 13 were waited for; matrix products, arithmetic and copies ran while one was open for 4% of the time, Pallas kernels for 66%

profile of v1, /device:TPU:0, one launch (start us, length us, event | category | flops | bytes accessed | tf_op | source)
XLA Modules:
  0.0 1977.4 jit_solution(16802677233074094299)
XLA Ops:
  3.3 8.8 fusion.2
  12.2 7.8 dynamic-slice_bitcast_fusion
  23.2 8.6 fusion.3
  31.9 11.7 slice_bitcast_fusion.1
  58.3 20.6 %collective-permute-done.2 = bf16[256,2560]{1,0:T(8,128)(2,1)} collective-permute-done((bf16[256,2560]{1,0:T(8,128)(2,1)}, bf16[256,2560]{1,0:T(8,128)(2,1)}, u32[]{:S(2)}, u32[]{:S(2)}) %collective-permute-start.2) | collective-permute-done | bytes 1310752 | tf_op jit(solution)/shard_map/ppermute | solution.py:320
  81.3 27.0 %collective-permute-done.38 = bf16[256,2560]{1,0:T(8,128)(2,1)} collective-permute-done((bf16[256,2560]{1,0:T(8,128)(2,1)}, bf16[256,2560]{1,0:T(8,128)(2,1)}, u32[]{:S(2)}, u32[]{:S(2)}) %collective-permute-start.38) | collective-permute-done | bytes 1310752 | tf_op jit(solution)/shard_map/ppermute | solution.py:320
  108.4 26.7 %collective-permute-done.39 = bf16[256,2560]{1,0:T(8,128)(2,1)} collective-permute-done((bf16[256,2560]{1,0:T(8,128)(2,1)}, bf16[256,2560]{1,0:T(8,128)(2,1)}, u32[]{:S(2)}, u32[]{:S(2)}) %collective-permute-start.39) | collective-permute-done | bytes 1310752 | tf_op jit(solution)/shard_map/ppermute | solution.py:320
  138.8 32.8 %collective-permute-done.14 = bf16[320,2560]{1,0:T(8,128)(2,1)} collective-permute-done((bf16[320,2560]{1,0:T(8,128)(2,1)}, bf16[320,2560]{1,0:T(8,128)(2,1)}, u32[]{:S(2)}, u32[]{:S(2)}) %collective-permute-start.14) | collective-permute-done | bytes 1638432 | tf_op jit(solution)/shard_map/ppermute | solution.py:320
  174.1 31.9 %collective-permute-done.28 = bf16[320,2560]{1,0:T(8,128)(2,1)} collective-permute-done((bf16[320,2560]{1,0:T(8,128)(2,1)S(1)}, bf16[320,2560]{1,0:T(8,128)(2,1)}, u32[]{:S(2)}, u32[]{:S(2)}) %collective-permute-start.28) | collective-permute-done | bytes 1638432 | tf_op jit(solution)/shard_map/ppermute | solution.py:320
  208.5 8.6 shard_map.123.h_ref
  226.3 8.6 shard_map.100.h_ref
  249.8 16.4 shard_map.124
  266.2 16.4 shard_map.101
  282.6 53.2 %collective-permute-done.40.h_ref = bf16[1024,2560]{1,0:T(8,128)(2,1)} collective-permute-done((bf16[1024,2560]{1,0:T(8,128)(2,1)}, bf16[1024,2560]{1,0:T(8,128)(2,1)}, u32[]{:S(2)}, u32[]{:S(2)}) %collective-permute-start.40) | collective-permute-done | bytes 5242912 | tf_op jit(solution)/shard_map/ppermute | solution.py:320
  336.1 16.7 shard_map.126
  352.8 94.9 %collective-permute-done.6.h_ref = bf16[1024,2560]{1,0:T(8,128)(2,1)} collective-permute-done((bf16[1024,2560]{1,0:T(8,128)(2,1)}, bf16[1024,2560]{1,0:T(8,128)(2,1)}, u32[]{:S(2)}, u32[]{:S(2)}) %collective-permute-start.6) | collective-permute-done | bytes 5242912 | tf_op jit(solution)/shard_map/ppermute | solution.py:320
  447.7 16.3 shard_map.103
  464.6 22.7 %shard_map.132 = (bf16[1024,1280]{1,0:T(8,128)(2,1)}, bf16[1024,1280]{1,0:T(8,128)(2,1)}) custom-call(bf16[1024,2560]{1,0:T(8,128)(2,1)} %collective-permute-done.40.h_ref, bf16[2560,1280]{1,0:T(8,128)(2,1)} %get-tuple-element.184.refs_0_, bf16[2560,1280]{1,0:T(8,128)(2,1)} %collective-permute-done.7.refs_1_, f32[1,1280]{1,0:T(1,128)} %get-tuple-element.217.refs_2_, ...), custom_call_target="tpu_custom_call" | custom-call | flops 13421772800 | bytes 23592960 | tf_op jit(solution)/shard_map/pallas_call | solution.py:231
  487.3 22.7 %shard_map.129 = (bf16[1024,1280]{1,0:T(8,128)(2,1)}, bf16[1024,1280]{1,0:T(8,128)(2,1)}) custom-call(bf16[1024,2560]{1,0:T(8,128)(2,1)} %shard_map.123.h_ref, bf16[2560,1280]{1,0:T(8,128)(2,1)} %get-tuple-element.184.refs_0_, bf16[2560,1280]{1,0:T(8,128)(2,1)} %collective-permute-done.7.refs_1_, f32[1,1280]{1,0:T(1,128)} %get-tuple-element.217.refs_2_, ...), custom_call_target="tpu_custom_call" | custom-call | flops 13421772800 | bytes 23592960 | tf_op jit(solution)/shard_map/pallas_call | solution.py:231
  510.0 23.3 %shard_map.109 = (bf16[1024,1280]{1,0:T(8,128)(2,1)}, bf16[1024,1280]{1,0:T(8,128)(2,1)}) custom-call(bf16[1024,2560]{1,0:T(8,128)(2,1)} %collective-permute-done.6.h_ref, bf16[2560,1280]{1,0:T(8,128)(2,1)} %get-tuple-element.184.refs_0_, bf16[2560,1280]{1,0:T(8,128)(2,1)} %collective-permute-done.7.refs_1_, f32[1,1280]{1,0:T(1,128)} %get-tuple-element.217.refs_2_, ...), custom_call_target="tpu_custom_call" | custom-call | flops 13421772800 | bytes 23592960 | tf_op jit(solution)/shard_map/pallas_call | solution.py:231
  533.3 22.7 %shard_map.106 = (bf16[1024,1280]{1,0:T(8,128)(2,1)}, bf16[1024,1280]{1,0:T(8,128)(2,1)}) custom-call(bf16[1024,2560]{1,0:T(8,128)(2,1)} %shard_map.100.h_ref, bf16[2560,1280]{1,0:T(8,128)(2,1)} %get-tuple-element.184.refs_0_, bf16[2560,1280]{1,0:T(8,128)(2,1)} %collective-permute-done.7.refs_1_, f32[1,1280]{1,0:T(1,128)} %get-tuple-element.217.refs_2_, ...), custom_call_target="tpu_custom_call" | custom-call | flops 13421772800 | bytes 23592960 | tf_op jit(solution)/shard_map/pallas_call | solution.py:231
  557.7 68.4 %collective-permute-done.17.refs_8_ = bf16[1280,2560]{1,0:T(8,128)(2,1)} collective-permute-done((bf16[1280,2560]{1,0:T(8,128)(2,1)}, bf16[1280,2560]{1,0:T(8,128)(2,1)}, u32[]{:S(2)}, u32[]{:S(2)}) %collective-permute-start.17) | collective-permute-done | bytes 6553632 | tf_op jit(solution)/shard_map/ppermute | solution.py:320
  626.6 16.4 shard_map.127
  643.0 16.3 shard_map.125
  659.3 16.6 shard_map.104
  675.9 16.4 shard_map.102
  692.3 63.0 %shard_map.128 = (bf16[1024,1280]{1,0:T(8,128)(2,1)}, bf16[1024,1280]{1,0:T(8,128)(2,1)}) custom-call(s32[8]{0:T(128)} %stack.35.pos_ref, bf16[960,1024]{1,0:T(8,128)(2,1)} %get-tuple-element.143.refs_0_, bf16[960,1024]{1,0:T(8,128)(2,1)} %get-tuple-element.144.refs_1_, bf16[960,1024]{1,0:T(8,128)(2,1)} %get-tuple-element.145.refs_2_, ...), custom_call_target="tpu_custom_call" | custom-call | flops 26843545600 | bytes 20971520 | tf_op jit(solution)/shard_map/pallas_call | solution.py:101
  755.3 62.8 %shard_map.105 = (bf16[1024,1280]{1,0:T(8,128)(2,1)}, bf16[1024,1280]{1,0:T(8,128)(2,1)}) custom-call(s32[8]{0:T(128)} %stack.35.pos_ref, bf16[960,1024]{1,0:T(8,128)(2,1)} %get-tuple-element.98.refs_0_, bf16[960,1024]{1,0:T(8,128)(2,1)} %get-tuple-element.99.refs_1_, bf16[960,1024]{1,0:T(8,128)(2,1)} %get-tuple-element.100.refs_2_, ...), custom_call_target="tpu_custom_call" | custom-call | flops 26843545600 | bytes 20971520 | tf_op jit(solution)/shard_map/pallas_call | solution.py:101
  818.4 23.1 %shard_map.110 = (bf16[1024,1280]{1,0:T(8,128)(2,1)}, bf16[1024,1280]{1,0:T(8,128)(2,1)}) custom-call(bf16[1024,2560]{1,0:T(8,128)(2,1)} %collective-permute-done.6.h_ref, bf16[2560,1280]{1,0:T(8,128)(2,1)} %collective-permute-done.9.refs_0_, bf16[2560,1280]{1,0:T(8,128)(2,1)} %collective-permute-done.10.refs_1_, f32[1,1280]{1,0:T(1,128)} %get-tuple-element.213.refs_2_, ...), custom_call_target="tpu_custom_call" | custom-call | flops 13421772800 | bytes 23592960 | tf_op jit(solution)/shard_map/pallas_call | solution.py:231
  841.5 44.2 %shard_map.111 = bf16[1024,2560]{1,0:T(8,128)(2,1)} custom-call(bf16[1024,1280]{1,0:T(8,128)(2,1)} %get-tuple-element.114.refs_0_, bf16[1024,1280]{1,0:T(8,128)(2,1)} %get-tuple-element.115.refs_1_, bf16[1024,1280]{1,0:T(8,128)(2,1)} %get-tuple-element.116.refs_2_, bf16[1024,1280]{1,0:T(8,128)(2,1)} %get-tuple-element.117.refs_3_, ...), custom_call_target="tpu_custom_call" | custom-call | flops 33554432000 | bytes 56360960 | tf_op jit(solution)/shard_map/pallas_call | solution.py:159
  887.3 22.7 %shard_map.133 = (bf16[1024,1280]{1,0:T(8,128)(2,1)}, bf16[1024,1280]{1,0:T(8,128)(2,1)}) custom-call(bf16[1024,2560]{1,0:T(8,128)(2,1)} %collective-permute-done.40.h_ref, bf16[2560,1280]{1,0:T(8,128)(2,1)} %collective-permute-done.9.refs_0_, bf16[2560,1280]{1,0:T(8,128)(2,1)} %collective-permute-done.10.refs_1_, f32[1,1280]{1,0:T(1,128)} %get-tuple-element.213.refs_2_, ...), custom_call_target="tpu_custom_call" | custom-call | flops 13421772800 | bytes 23592960 | tf_op jit(solution)/shard_map/pallas_call | solution.py:231
  910.0 44.3 %shard_map.134 = bf16[1024,2560]{1,0:T(8,128)(2,1)} custom-call(bf16[1024,1280]{1,0:T(8,128)(2,1)} %get-tuple-element.156.refs_0_, bf16[1024,1280]{1,0:T(8,128)(2,1)} %get-tuple-element.157.refs_1_, bf16[1024,1280]{1,0:T(8,128)(2,1)} %get-tuple-element.158.refs_2_, bf16[1024,1280]{1,0:T(8,128)(2,1)} %get-tuple-element.159.refs_3_, ...), custom_call_target="tpu_custom_call" | custom-call | flops 33554432000 | bytes 56360960 | tf_op jit(solution)/shard_map/pallas_call | solution.py:159
  954.8 22.7 %shard_map.130 = (bf16[1024,1280]{1,0:T(8,128)(2,1)}, bf16[1024,1280]{1,0:T(8,128)(2,1)}) custom-call(bf16[1024,2560]{1,0:T(8,128)(2,1)} %shard_map.123.h_ref, bf16[2560,1280]{1,0:T(8,128)(2,1)} %collective-permute-done.9.refs_0_, bf16[2560,1280]{1,0:T(8,128)(2,1)} %collective-permute-done.10.refs_1_, f32[1,1280]{1,0:T(1,128)} %get-tuple-element.213.refs_2_, ...), custom_call_target="tpu_custom_call" | custom-call | flops 13421772800 | bytes 23592960 | tf_op jit(solution)/shard_map/pallas_call | solution.py:231
  977.5 44.4 %shard_map.131.kept = f32[1024,2560]{1,0:T(8,128)} custom-call(bf16[1024,1280]{1,0:T(8,128)(2,1)} %get-tuple-element.151.refs_0_, bf16[1024,1280]{1,0:T(8,128)(2,1)} %get-tuple-element.152.refs_1_, bf16[1024,1280]{1,0:T(8,128)(2,1)} %get-tuple-element.153.refs_2_, bf16[1024,1280]{1,0:T(8,128)(2,1)} %get-tuple-element.154.refs_3_, ...), custom_call_target="tpu_custom_call" | custom-call | flops 33554432000 | bytes 56360960 | tf_op jit(solution)/shard_map/pallas_call | solution.py:159
  1021.9 22.9 %shard_map.107 = (bf16[1024,1280]{1,0:T(8,128)(2,1)}, bf16[1024,1280]{1,0:T(8,128)(2,1)}) custom-call(bf16[1024,2560]{1,0:T(8,128)(2,1)} %shard_map.100.h_ref, bf16[2560,1280]{1,0:T(8,128)(2,1)} %collective-permute-done.9.refs_0_, bf16[2560,1280]{1,0:T(8,128)(2,1)} %collective-permute-done.10.refs_1_, f32[1,1280]{1,0:T(1,128)} %get-tuple-element.213.refs_2_, ...), custom_call_target="tpu_custom_call" | custom-call | flops 13421772800 | bytes 23592960 | tf_op jit(solution)/shard_map/pallas_call | solution.py:231
  1045.4 68.4 %collective-permute-done.41.received = bf16[1024,2560]{1,0:T(8,128)(2,1)} collective-permute-done((bf16[1024,2560]{1,0:T(8,128)(2,1)}, bf16[1024,2560]{1,0:T(8,128)(2,1)}, u32[]{:S(2)}, u32[]{:S(2)}) %collective-permute-start.41) | collective-permute-done | bytes 5242912 | tf_op jit(solution)/shard_map/ppermute | solution.py:320
  1113.8 44.3 %shard_map.108.kept = f32[1024,2560]{1,0:T(8,128)} custom-call(bf16[1024,1280]{1,0:T(8,128)(2,1)} %get-tuple-element.106.refs_0_, bf16[1024,1280]{1,0:T(8,128)(2,1)} %get-tuple-element.108.refs_1_, bf16[1024,1280]{1,0:T(8,128)(2,1)} %get-tuple-element.109.refs_2_, bf16[1024,1280]{1,0:T(8,128)(2,1)} %get-tuple-element.110.refs_3_, ...), custom_call_target="tpu_custom_call" | custom-call | flops 33554432000 | bytes 56360960 | tf_op jit(solution)/shard_map/pallas_call | solution.py:159
  1158.1 15.4 shard_map.112
  1173.5 15.3 shard_map.135
  1189.3 16.4 shard_map.114
  1205.7 16.7 shard_map.137
  1224.1 16.4 shard_map.113
  1240.5 16.3 shard_map.136
  1257.2 43.8 %shard_map.141 = (bf16[1024,1280]{1,0:T(8,128)(2,1)}, bf16[1024,1280]{1,0:T(8,128)(2,1)}, bf16[1024,1280]{1,0:T(8,128)(2,1)}, bf16[1024,1280]{1,0:T(8,128)(2,1)}) custom-call(bf16[1024,2560]{1,0:T(8,128)(2,1)} %get-tuple-element.162.h_ref, bf16[2560,1280]{1,0:T(8,128)(2,1)} %get-tuple-element.183.refs_0_, ...), custom_call_target="tpu_custom_call" | custom-call | flops 26843545600 | bytes 41943040 | tf_op jit(solution)/shard_map/pallas_call | solution.py:231
  1301.0 43.6 %shard_map.118 = (bf16[1024,1280]{1,0:T(8,128)(2,1)}, bf16[1024,1280]{1,0:T(8,128)(2,1)}, bf16[1024,1280]{1,0:T(8,128)(2,1)}, bf16[1024,1280]{1,0:T(8,128)(2,1)}) custom-call(bf16[1024,2560]{1,0:T(8,128)(2,1)} %get-tuple-element.120.h_ref, bf16[2560,1280]{1,0:T(8,128)(2,1)} %get-tuple-element.183.refs_0_, ...), custom_call_target="tpu_custom_call" | custom-call | flops 26843545600 | bytes 41943040 | tf_op jit(solution)/shard_map/pallas_call | solution.py:231
  1344.6 16.4 shard_map.139
  1361.0 16.6 shard_map.138
  1377.5 62.8 %shard_map.140 = (bf16[1024,1280]{1,0:T(8,128)(2,1)}, bf16[1024,1280]{1,0:T(8,128)(2,1)}) custom-call(s32[8]{0:T(128)} %stack.35.pos_ref, bf16[960,1024]{1,0:T(8,128)(2,1)} %get-tuple-element.163.refs_0_, bf16[960,1024]{1,0:T(8,128)(2,1)} %get-tuple-element.164.refs_1_, bf16[960,1024]{1,0:T(8,128)(2,1)} %get-tuple-element.165.refs_2_, ...), custom_call_target="tpu_custom_call" | custom-call | flops 26843545600 | bytes 20971520 | tf_op jit(solution)/shard_map/pallas_call | solution.py:101
  1440.4 44.0 %shard_map.143 = (bf16[1024,1280]{1,0:T(8,128)(2,1)}, bf16[1024,1280]{1,0:T(8,128)(2,1)}, bf16[1024,1280]{1,0:T(8,128)(2,1)}, bf16[1024,1280]{1,0:T(8,128)(2,1)}) custom-call(bf16[1024,2560]{1,0:T(8,128)(2,1)} %collective-permute-done.42.h_ref, bf16[2560,1280]{1,0:T(8,128)(2,1)} %get-tuple-element.183.refs_0_, ...), custom_call_target="tpu_custom_call" | custom-call | flops 26843545600 | bytes 41943040 | tf_op jit(solution)/shard_map/pallas_call | solution.py:231
  1484.4 25.8 %shard_map.144 = bf16[512,2560]{1,0:T(8,128)(2,1)} custom-call(bf16[1024,1280]{1,0:T(8,128)(2,1)} %get-tuple-element.176.refs_0_, bf16[1024,1280]{1,0:T(8,128)(2,1)} %get-tuple-element.177.refs_1_, bf16[1024,1280]{1,0:T(8,128)(2,1)} %get-tuple-element.178.refs_2_, bf16[1024,1280]{1,0:T(8,128)(2,1)} %get-tuple-element.179.refs_3_, ...), custom_call_target="tpu_custom_call" | custom-call | flops 16777216000 | bytes 44564480 | tf_op jit(solution)/shard_map/pallas_call | solution.py:159
  1511.8 25.8 %shard_map.147 = bf16[512,2560]{1,0:T(8,128)(2,1)} custom-call(bf16[1024,1280]{1,0:T(8,128)(2,1)} %get-tuple-element.176.refs_0_, bf16[1024,1280]{1,0:T(8,128)(2,1)} %get-tuple-element.177.refs_1_, bf16[1024,1280]{1,0:T(8,128)(2,1)} %get-tuple-element.178.refs_2_, bf16[1024,1280]{1,0:T(8,128)(2,1)} %get-tuple-element.179.refs_3_, ...), custom_call_target="tpu_custom_call" | custom-call | flops 16777216000 | bytes 44564480 | tf_op jit(solution)/shard_map/pallas_call | solution.py:159
  1538.1 16.6 shard_map.116
  1554.6 16.4 shard_map.115
  1571.0 63.1 %shard_map.117 = (bf16[1024,1280]{1,0:T(8,128)(2,1)}, bf16[1024,1280]{1,0:T(8,128)(2,1)}) custom-call(s32[8]{0:T(128)} %stack.35.pos_ref, bf16[960,1024]{1,0:T(8,128)(2,1)} %get-tuple-element.121.refs_0_, bf16[960,1024]{1,0:T(8,128)(2,1)} %get-tuple-element.122.refs_1_, bf16[960,1024]{1,0:T(8,128)(2,1)} %get-tuple-element.123.refs_2_, ...), custom_call_target="tpu_custom_call" | custom-call | flops 26843545600 | bytes 20971520 | tf_op jit(solution)/shard_map/pallas_call | solution.py:101
  1634.1 43.6 %shard_map.120 = (bf16[1024,1280]{1,0:T(8,128)(2,1)}, bf16[1024,1280]{1,0:T(8,128)(2,1)}, bf16[1024,1280]{1,0:T(8,128)(2,1)}, bf16[1024,1280]{1,0:T(8,128)(2,1)}) custom-call(bf16[1024,2560]{1,0:T(8,128)(2,1)} %collective-permute-done.23.h_ref, bf16[2560,1280]{1,0:T(8,128)(2,1)} %get-tuple-element.183.refs_0_, ...), custom_call_target="tpu_custom_call" | custom-call | flops 26843545600 | bytes 41943040 | tf_op jit(solution)/shard_map/pallas_call | solution.py:231
  1677.7 44.5 %shard_map.121 = bf16[1024,2560]{1,0:T(8,128)(2,1)} custom-call(bf16[1024,1280]{1,0:T(8,128)(2,1)} %get-tuple-element.134.refs_0_, bf16[1024,1280]{1,0:T(8,128)(2,1)} %get-tuple-element.135.refs_1_, bf16[1024,1280]{1,0:T(8,128)(2,1)} %get-tuple-element.136.refs_2_, bf16[1024,1280]{1,0:T(8,128)(2,1)} %get-tuple-element.137.refs_3_, ...), custom_call_target="tpu_custom_call" | custom-call | flops 33554432000 | bytes 56360960 | tf_op jit(solution)/shard_map/pallas_call | solution.py:159
  1723.7 26.3 %shard_map.146.kept = f32[512,2560]{1,0:T(8,128)} custom-call(bf16[1024,1280]{1,0:T(8,128)(2,1)} %get-tuple-element.171.refs_0_, bf16[1024,1280]{1,0:T(8,128)(2,1)} %get-tuple-element.172.refs_1_, bf16[1024,1280]{1,0:T(8,128)(2,1)} %get-tuple-element.173.refs_2_, bf16[1024,1280]{1,0:T(8,128)(2,1)} %get-tuple-element.174.refs_3_, ...), custom_call_target="tpu_custom_call" | custom-call | flops 16777216000 | bytes 44564480 | tf_op jit(solution)/shard_map/pallas_call | solution.py:159
  1750.0 26.3 %shard_map.142.kept = f32[512,2560]{1,0:T(8,128)} custom-call(bf16[1024,1280]{1,0:T(8,128)(2,1)} %get-tuple-element.171.refs_0_, bf16[1024,1280]{1,0:T(8,128)(2,1)} %get-tuple-element.172.refs_1_, bf16[1024,1280]{1,0:T(8,128)(2,1)} %get-tuple-element.173.refs_2_, bf16[1024,1280]{1,0:T(8,128)(2,1)} %get-tuple-element.174.refs_3_, ...), custom_call_target="tpu_custom_call" | custom-call | flops 16777216000 | bytes 44564480 | tf_op jit(solution)/shard_map/pallas_call | solution.py:159
  1776.2 44.8 %shard_map.119.kept = f32[1024,2560]{1,0:T(8,128)} custom-call(bf16[1024,1280]{1,0:T(8,128)(2,1)} %get-tuple-element.129.refs_0_, bf16[1024,1280]{1,0:T(8,128)(2,1)} %get-tuple-element.130.refs_1_, bf16[1024,1280]{1,0:T(8,128)(2,1)} %get-tuple-element.131.refs_2_, bf16[1024,1280]{1,0:T(8,128)(2,1)} %get-tuple-element.132.refs_3_, ...), custom_call_target="tpu_custom_call" | custom-call | flops 33554432000 | bytes 56360960 | tf_op jit(solution)/shard_map/pallas_call | solution.py:159
  1821.0 7.3 shard_map.145
  1829.7 6.8 shard_map.148
  1836.7 12.4 shard_map.122
  1861.7 80.0 %collective-permute-done.35 = bf16[256,2560]{1,0:T(8,128)(2,1)} collective-permute-done((bf16[256,2560]{1,0:T(8,128)(2,1)}, bf16[256,2560]{1,0:T(8,128)(2,1)}, u32[]{:S(2)}, u32[]{:S(2)}) %collective-permute-start.35) | collective-permute-done | bytes 1310752 | tf_op jit(solution)/shard_map/ppermute | solution.py:320
  1943.1 25.4 %collective-permute-done.36 = bf16[256,2560]{1,0:T(8,128)(2,1)S(1)} collective-permute-done((bf16[256,2560]{1,0:T(8,128)(2,1)S(1)}, bf16[256,2560]{1,0:T(8,128)(2,1)S(1)}, u32[]{:S(2)}, u32[]{:S(2)}) %collective-permute-start.36) | collective-permute-done | bytes 1310752 | tf_op jit(solution)/shard_map/ppermute | solution.py:320
  (147 shorter events, 92.9 us)
Async XLA Ops:
  0.0 49.9 %collective-permute-start.8 = (f32[2,1280]{1,0:T(2,128)}, f32[2,1280]{1,0:T(2,128)S(1)}, u32[]{:S(2)}, u32[]{:S(2)}) collective-permute-start(f32[2,1280]{1,0:T(2,128)} %param.17), channel_id=1, source_target_pairs={{0,1},{1,0},{2,3},{3,2},{4,5},{5,4},{6,7},{7,6}} | collective-permute-start | bytes 30728 | tf_op jit(solution)/shard_map/ppermute | solution.py:320
  0.8 49.5 %collective-permute-start.11 = (f32[2,1280]{1,0:T(2,128)}, f32[2,1280]{1,0:T(2,128)S(1)}, u32[]{:S(2)}, u32[]{:S(2)}) collective-permute-start(f32[2,1280]{1,0:T(2,128)} %param.17), channel_id=1, source_target_pairs={{0,4},{1,5},{2,6},{3,7},{4,0},{5,1},{6,2},{7,3}} | collective-permute-start | bytes 30728 | tf_op jit(solution)/shard_map/ppermute | solution.py:320
  12.2 9.7 copy-start.4
  20.0 33.7 %collective-permute-start = (bf16[256,2560]{1,0:T(8,128)(2,1)}, bf16[256,2560]{1,0:T(8,128)(2,1)}, u32[]{:S(2)}, u32[]{:S(2)}) collective-permute-start(bf16[256,2560]{1,0:T(8,128)(2,1)} %get-tuple-element.94), channel_id=1, source_target_pairs={{0,1},{1,0},{2,3},{3,2},{4,5},{5,4},{6,7},{7,6}} | collective-permute-start | bytes 3932168 | tf_op jit(solution)/shard_map/ppermute | solution.py:320
  20.2 36.6 %collective-permute-start.1 = (bf16[256,2560]{1,0:T(8,128)(2,1)}, bf16[256,2560]{1,0:T(8,128)(2,1)}, u32[]{:S(2)}, u32[]{:S(2)}) collective-permute-start(bf16[256,2560]{1,0:T(8,128)(2,1)} %get-tuple-element.95), channel_id=1, source_target_pairs={{0,4},{1,5},{2,6},{3,7},{4,0},{5,1},{6,2},{7,3}} | collective-permute-start | bytes 3932168 | tf_op jit(solution)/shard_map/ppermute | solution.py:320
  20.5 58.4 %collective-permute-start.2 = (bf16[256,2560]{1,0:T(8,128)(2,1)}, bf16[256,2560]{1,0:T(8,128)(2,1)}, u32[]{:S(2)}, u32[]{:S(2)}) collective-permute-start(bf16[256,2560]{1,0:T(8,128)(2,1)} %get-tuple-element.96), channel_id=1, source_target_pairs={{0,5},{1,4},{2,7},{3,6},{4,1},{5,0},{6,3},{7,2}} | collective-permute-start | bytes 3932168 | tf_op jit(solution)/shard_map/ppermute | solution.py:320
  23.2 20.3 %slice-start = ((s8[13107200]{0:T(1024)(128)(4,1)}), s8[524288]{0:T(1024)(128)(4,1)S(1)}, s32[]{:S(2)}) async-start(s8[13107200]{0:T(1024)(128)(4,1)} %bitcast.66), calls=%async_computation | async-start | bytes 1048576
  23.2 20.3 %slice-start.1 = ((s8[13107200]{0:T(1024)(128)(4,1)}), s8[4194304]{0:T(1024)(128)(4,1)S(1)}, s32[]{:S(2)}) async-start(s8[13107200]{0:T(1024)(128)(4,1)} %bitcast.66), calls=%async_computation.1 | async-start | bytes 8388608
  31.8 11.7 slice-start.2
  31.9 11.7 slice-start.3
  43.6 5.0 copy-start.6
  43.6 5.0 copy-start.7
  43.6 5.7 copy-start.8
  43.6 5.7 copy-start.9
  43.6 6.8 copy-start.10
  43.6 11.5 copy-start.3
  49.9 30.6 %collective-permute-start.37 = (bf16[256,2560]{1,0:T(8,128)(2,1)}, bf16[256,2560]{1,0:T(8,128)(2,1)}, u32[]{:S(2)}, u32[]{:S(2)}) collective-permute-start(bf16[256,2560]{1,0:T(8,128)(2,1)} %get-tuple-element.140), channel_id=1, source_target_pairs={{0,1},{1,0},{2,3},{3,2},{4,5},{5,4},{6,7},{7,6}} | collective-permute-start | bytes 3932168 | tf_op jit(solution)/shard_map/ppermute | solution.py:320
  50.4 3.0 collective-permute-start.12
  53.4 55.0 %collective-permute-start.38 = (bf16[256,2560]{1,0:T(8,128)(2,1)}, bf16[256,2560]{1,0:T(8,128)(2,1)}, u32[]{:S(2)}, u32[]{:S(2)}) collective-permute-start(bf16[256,2560]{1,0:T(8,128)(2,1)} %get-tuple-element.141), channel_id=1, source_target_pairs={{0,4},{1,5},{2,6},{3,7},{4,0},{5,1},{6,2},{7,3}} | collective-permute-start | bytes 3932168 | tf_op jit(solution)/shard_map/ppermute | solution.py:320
  53.7 81.4 %collective-permute-start.39 = (bf16[256,2560]{1,0:T(8,128)(2,1)}, bf16[256,2560]{1,0:T(8,128)(2,1)}, u32[]{:S(2)}, u32[]{:S(2)}) collective-permute-start(bf16[256,2560]{1,0:T(8,128)(2,1)} %get-tuple-element.142), channel_id=1, source_target_pairs={{0,5},{1,4},{2,7},{3,6},{4,1},{5,0},{6,3},{7,2}} | collective-permute-start | bytes 3932168 | tf_op jit(solution)/shard_map/ppermute | solution.py:320
  56.9 114.7 %collective-permute-start.14 = (bf16[320,2560]{1,0:T(8,128)(2,1)}, bf16[320,2560]{1,0:T(8,128)(2,1)}, u32[]{:S(2)}, u32[]{:S(2)}) collective-permute-start(bf16[320,2560]{1,0:T(8,128)(2,1)} %bitcast.72), channel_id=1, source_target_pairs={{0,4},{1,5},{2,6},{3,7},{4,0},{5,1},{6,2},{7,3}} | collective-permute-start | bytes 4915208 | tf_op jit(solution)/shard_map/ppermute | solution.py:320
  78.9 127.1 %collective-permute-start.28 = (bf16[320,2560]{1,0:T(8,128)(2,1)S(1)}, bf16[320,2560]{1,0:T(8,128)(2,1)}, u32[]{:S(2)}, u32[]{:S(2)}) collective-permute-start(bf16[320,2560]{1,0:T(8,128)(2,1)S(1)} %bitcast.69), channel_id=1, source_target_pairs={{0,4},{1,5},{2,6},{3,7},{4,0},{5,1},{6,2},{7,3}} | collective-permute-start | bytes 4915208 | tf_op jit(solution)/shard_map/ppermute | solution.py:320
  80.4 139.2 %collective-permute-start.13 = (bf16[320,2560]{1,0:T(8,128)(2,1)}, bf16[320,2560]{1,0:T(8,128)(2,1)}, u32[]{:S(2)}, u32[]{:S(2)}) collective-permute-start(bf16[320,2560]{1,0:T(8,128)(2,1)} %bitcast.73), channel_id=1, source_target_pairs={{0,1},{1,0},{2,3},{3,2},{4,5},{5,4},{6,7},{7,6}} | collective-permute-start | bytes 4915208 | tf_op jit(solution)/shard_map/ppermute | solution.py:320
  108.4 115.2 %collective-permute-start.27 = (bf16[320,2560]{1,0:T(8,128)(2,1)S(1)}, bf16[320,2560]{1,0:T(8,128)(2,1)}, u32[]{:S(2)}, u32[]{:S(2)}) collective-permute-start(bf16[320,2560]{1,0:T(8,128)(2,1)S(1)} %bitcast.70), channel_id=1, source_target_pairs={{0,1},{1,0},{2,3},{3,2},{4,5},{5,4},{6,7},{7,6}} | collective-permute-start | bytes 4915208 | tf_op jit(solution)/shard_map/ppermute | solution.py:320
  135.1 113.0 %collective-permute-start.3 = (bf16[960,2560]{1,0:T(8,128)(2,1)}, bf16[960,2560]{1,0:T(8,128)(2,1)}, u32[]{:S(2)}, u32[]{:S(2)}) collective-permute-start(bf16[960,2560]{1,0:T(8,128)(2,1)} %bitcast.81), channel_id=1, source_target_pairs={{0,1},{1,0},{2,3},{3,2},{4,5},{5,4},{6,7},{7,6}} | collective-permute-start | bytes 14745608 | tf_op jit(solution)/shard_map/ppermute | solution.py:320
  171.6 63.3 %collective-permute-start.15 = (bf16[320,2560]{1,0:T(8,128)(2,1)}, bf16[320,2560]{1,0:T(8,128)(2,1)}, u32[]{:S(2)}, u32[]{:S(2)}) collective-permute-start(bf16[320,2560]{1,0:T(8,128)(2,1)} %collective-permute-done.14), channel_id=1, source_target_pairs={{0,1},{1,0},{2,3},{3,2},{4,5},{5,4},{6,7},{7,6}} | collective-permute-start | bytes 4915208 | tf_op jit(solution)/shard_map/ppermute | solution.py:320
  206.0 30.0 %collective-permute-start.29 = (bf16[320,2560]{1,0:T(8,128)(2,1)}, bf16[320,2560]{1,0:T(8,128)(2,1)}, u32[]{:S(2)}, u32[]{:S(2)}) collective-permute-start(bf16[320,2560]{1,0:T(8,128)(2,1)} %collective-permute-done.28), channel_id=1, source_target_pairs={{0,1},{1,0},{2,3},{3,2},{4,5},{5,4},{6,7},{7,6}} | collective-permute-start | bytes 4915208 | tf_op jit(solution)/shard_map/ppermute | solution.py:320
  219.6 116.2 %collective-permute-start.40 = (bf16[1024,2560]{1,0:T(8,128)(2,1)}, bf16[1024,2560]{1,0:T(8,128)(2,1)}, u32[]{:S(2)}, u32[]{:S(2)}) collective-permute-start(bf16[1024,2560]{1,0:T(8,128)(2,1)} %shard_map.123.h_ref), channel_id=1, source_target_pairs={{0,2},{1,3},{2,0},{3,1},{4,6},{5,7},{6,4},{7,5}} | collective-permute-start | bytes 15728648 | tf_op jit(solution)/shard_map/ppermute | solution.py:320
  223.6 240.8 %collective-permute-start.7 = (bf16[2560,1280]{1,0:T(8,128)(2,1)}, bf16[2560,1280]{1,0:T(8,128)(2,1)}, u32[]{:S(2)}, u32[]{:S(2)}) collective-permute-start(bf16[2560,1280]{1,0:T(8,128)(2,1)} %get-tuple-element.184.refs_0_), channel_id=1, source_target_pairs={{0,1},{1,0},{2,3},{3,2},{4,5},{5,4},{6,7},{7,6}} | collective-permute-start | bytes 19660808 | tf_op jit(solution)/shard_map/ppermute | solution.py:320
  234.9 212.9 %collective-permute-start.6 = (bf16[1024,2560]{1,0:T(8,128)(2,1)}, bf16[1024,2560]{1,0:T(8,128)(2,1)}, u32[]{:S(2)}, u32[]{:S(2)}) collective-permute-start(bf16[1024,2560]{1,0:T(8,128)(2,1)} %shard_map.100.h_ref), channel_id=1, source_target_pairs={{0,2},{1,3},{2,0},{3,1},{4,6},{5,7},{6,4},{7,5}} | collective-permute-start | bytes 15728648 | tf_op jit(solution)/shard_map/ppermute | solution.py:320
  236.0 228.1 %collective-permute-start.4 = (bf16[960,2560]{1,0:T(8,128)(2,1)}, bf16[960,2560]{1,0:T(8,128)(2,1)}, u32[]{:S(2)}, u32[]{:S(2)}) collective-permute-start(bf16[960,2560]{1,0:T(8,128)(2,1)} %bitcast.82), channel_id=1, source_target_pairs={{0,4},{1,5},{2,6},{3,7},{4,0},{5,1},{6,2},{7,3}} | collective-permute-start | bytes 14745608 | tf_op jit(solution)/shard_map/ppermute | solution.py:320
  248.1 307.9 %collective-permute-start.9 = (bf16[2560,1280]{1,0:T(8,128)(2,1)}, bf16[2560,1280]{1,0:T(8,128)(2,1)}, u32[]{:S(2)}, u32[]{:S(2)}) collective-permute-start(bf16[2560,1280]{1,0:T(8,128)(2,1)} %get-tuple-element.184.refs_0_), channel_id=1, source_target_pairs={{0,4},{1,5},{2,6},{3,7},{4,0},{5,1},{6,2},{7,3}} | collective-permute-start | bytes 19660808 | tf_op jit(solution)/shard_map/ppermute | solution.py:320
  335.8 290.3 %collective-permute-start.17 = (bf16[1280,2560]{1,0:T(8,128)(2,1)}, bf16[1280,2560]{1,0:T(8,128)(2,1)}, u32[]{:S(2)}, u32[]{:S(2)}) collective-permute-start(bf16[1280,2560]{1,0:T(8,128)(2,1)} %get-tuple-element.182.refs_6_), channel_id=1, source_target_pairs={{0,4},{1,5},{2,6},{3,7},{4,0},{5,1},{6,2},{7,3}} | collective-permute-start | bytes 19660808 | tf_op jit(solution)/shard_map/ppermute | solution.py:320
  447.7 393.7 %collective-permute-start.16 = (bf16[1280,2560]{1,0:T(8,128)(2,1)}, bf16[1280,2560]{1,0:T(8,128)(2,1)}, u32[]{:S(2)}, u32[]{:S(2)}) collective-permute-start(bf16[1280,2560]{1,0:T(8,128)(2,1)} %get-tuple-element.182.refs_6_), channel_id=1, source_target_pairs={{0,1},{1,0},{2,3},{3,2},{4,5},{5,4},{6,7},{7,6}} | collective-permute-start | bytes 19660808 | tf_op jit(solution)/shard_map/ppermute | solution.py:320
  464.1 354.0 %collective-permute-start.21 = (bf16[960,2560]{1,0:T(8,128)(2,1)}, bf16[960,2560]{1,0:T(8,128)(2,1)}, u32[]{:S(2)}, u32[]{:S(2)}) collective-permute-start(bf16[960,2560]{1,0:T(8,128)(2,1)} %bitcast.75), channel_id=1, source_target_pairs={{0,4},{1,5},{2,6},{3,7},{4,0},{5,1},{6,2},{7,3}} | collective-permute-start | bytes 14745608 | tf_op jit(solution)/shard_map/ppermute | solution.py:320
  464.4 161.8 %collective-permute-start.5 = (bf16[960,2560]{1,0:T(8,128)(2,1)}, bf16[960,2560]{1,0:T(8,128)(2,1)}, u32[]{:S(2)}, u32[]{:S(2)}) collective-permute-start(bf16[960,2560]{1,0:T(8,128)(2,1)} %collective-permute-done.4.w_a), channel_id=1, source_target_pairs={{0,1},{1,0},{2,3},{3,2},{4,5},{5,4},{6,7},{7,6}} | collective-permute-start | bytes 14745608 | tf_op jit(solution)/shard_map/ppermute | solution.py:320
  556.0 488.8 %collective-permute-start.25 = (bf16[2560,1280]{1,0:T(8,128)(2,1)}, bf16[2560,1280]{1,0:T(8,128)(2,1)}, u32[]{:S(2)}, u32[]{:S(2)}) collective-permute-start(bf16[2560,1280]{1,0:T(8,128)(2,1)} %get-tuple-element.183.refs_0_), channel_id=1, source_target_pairs={{0,4},{1,5},{2,6},{3,7},{4,0},{5,1},{6,2},{7,3}} | collective-permute-start | bytes 19660808 | tf_op jit(solution)/shard_map/ppermute | solution.py:320
  626.1 192.2 %collective-permute-start.10 = (bf16[2560,1280]{1,0:T(8,128)(2,1)}, bf16[2560,1280]{1,0:T(8,128)(2,1)}, u32[]{:S(2)}, u32[]{:S(2)}) collective-permute-start(bf16[2560,1280]{1,0:T(8,128)(2,1)} %collective-permute-done.9.refs_0_), channel_id=1, source_target_pairs={{0,1},{1,0},{2,3},{3,2},{4,5},{5,4},{6,7},{7,6}} | collective-permute-start | bytes 19660808 | tf_op jit(solution)/shard_map/ppermute | solution.py:320
  626.1 215.3 %collective-permute-start.18 = (bf16[1280,2560]{1,0:T(8,128)(2,1)}, bf16[1280,2560]{1,0:T(8,128)(2,1)}, u32[]{:S(2)}, u32[]{:S(2)}) collective-permute-start(bf16[1280,2560]{1,0:T(8,128)(2,1)} %collective-permute-done.17.refs_8_), channel_id=1, source_target_pairs={{0,1},{1,0},{2,3},{3,2},{4,5},{5,4},{6,7},{7,6}} | collective-permute-start | bytes 19660808 | tf_op jit(solution)/shard_map/ppermute | solution.py:320
  818.1 370.7 %collective-permute-start.31 = (bf16[1280,2560]{1,0:T(8,128)(2,1)}, bf16[1280,2560]{1,0:T(8,128)(2,1)}, u32[]{:S(2)}, u32[]{:S(2)}) collective-permute-start(bf16[1280,2560]{1,0:T(8,128)(2,1)} %get-tuple-element.181.refs_6_), channel_id=1, source_target_pairs={{0,4},{1,5},{2,6},{3,7},{4,0},{5,1},{6,2},{7,3}} | collective-permute-start | bytes 19660808 | tf_op jit(solution)/shard_map/ppermute | solution.py:320
  818.4 370.9 %collective-permute-start.22 = (bf16[960,2560]{1,0:T(8,128)(2,1)}, bf16[960,2560]{1,0:T(8,128)(2,1)}, u32[]{:S(2)}, u32[]{:S(2)}) collective-permute-start(bf16[960,2560]{1,0:T(8,128)(2,1)} %collective-permute-done.21.w_a), channel_id=1, source_target_pairs={{0,1},{1,0},{2,3},{3,2},{4,5},{5,4},{6,7},{7,6}} | collective-permute-start | bytes 14745608 | tf_op jit(solution)/shard_map/ppermute | solution.py:320
  885.7 159.2 %collective-permute-start.19 = (bf16[1024,2560]{1,0:T(8,128)(2,1)}, bf16[1024,2560]{1,0:T(8,128)(2,1)}, u32[]{:S(2)}, u32[]{:S(2)}) collective-permute-start(bf16[1024,2560]{1,0:T(8,128)(2,1)} %shard_map.111), channel_id=1, source_target_pairs={{0,2},{1,3},{2,0},{3,1},{4,6},{5,7},{6,4},{7,5}} | collective-permute-start | bytes 15728648 | tf_op jit(solution)/shard_map/ppermute | solution.py:320
  954.4 159.4 %collective-permute-start.41 = (bf16[1024,2560]{1,0:T(8,128)(2,1)}, bf16[1024,2560]{1,0:T(8,128)(2,1)}, u32[]{:S(2)}, u32[]{:S(2)}) collective-permute-start(bf16[1024,2560]{1,0:T(8,128)(2,1)} %shard_map.134), channel_id=1, source_target_pairs={{0,2},{1,3},{2,0},{3,1},{4,6},{5,7},{6,4},{7,5}} | collective-permute-start | bytes 15728648 | tf_op jit(solution)/shard_map/ppermute | solution.py:320
  1044.8 177.7 %collective-permute-start.20 = (bf16[960,2560]{1,0:T(8,128)(2,1)}, bf16[960,2560]{1,0:T(8,128)(2,1)}, u32[]{:S(2)}, u32[]{:S(2)}) collective-permute-start(bf16[960,2560]{1,0:T(8,128)(2,1)} %bitcast.76), channel_id=1, source_target_pairs={{0,1},{1,0},{2,3},{3,2},{4,5},{5,4},{6,7},{7,6}} | collective-permute-start | bytes 14745608 | tf_op jit(solution)/shard_map/ppermute | solution.py:320
  1044.9 211.9 %collective-permute-start.24 = (bf16[2560,1280]{1,0:T(8,128)(2,1)}, bf16[2560,1280]{1,0:T(8,128)(2,1)}, u32[]{:S(2)}, u32[]{:S(2)}) collective-permute-start(bf16[2560,1280]{1,0:T(8,128)(2,1)} %get-tuple-element.183.refs_0_), channel_id=1, source_target_pairs={{0,1},{1,0},{2,3},{3,2},{4,5},{5,4},{6,7},{7,6}} | collective-permute-start | bytes 19660808 | tf_op jit(solution)/shard_map/ppermute | solution.py:320
  1113.8 143.4 %collective-permute-start.26 = (bf16[2560,1280]{1,0:T(8,128)(2,1)}, bf16[2560,1280]{1,0:T(8,128)(2,1)}, u32[]{:S(2)}, u32[]{:S(2)}) collective-permute-start(bf16[2560,1280]{1,0:T(8,128)(2,1)} %collective-permute-done.25.refs_2_), channel_id=1, source_target_pairs={{0,1},{1,0},{2,3},{3,2},{4,5},{5,4},{6,7},{7,6}} | collective-permute-start | bytes 19660808 | tf_op jit(solution)/shard_map/ppermute | solution.py:320
  1188.8 295.6 %collective-permute-start.30 = (bf16[1280,2560]{1,0:T(8,128)(2,1)}, bf16[1280,2560]{1,0:T(8,128)(2,1)}, u32[]{:S(2)}, u32[]{:S(2)}) collective-permute-start(bf16[1280,2560]{1,0:T(8,128)(2,1)} %get-tuple-element.181.refs_6_), channel_id=1, source_target_pairs={{0,1},{1,0},{2,3},{3,2},{4,5},{5,4},{6,7},{7,6}} | collective-permute-start | bytes 19660808 | tf_op jit(solution)/shard_map/ppermute | solution.py:320
  1189.3 295.1 %collective-permute-start.32 = (bf16[1280,2560]{1,0:T(8,128)(2,1)}, bf16[1280,2560]{1,0:T(8,128)(2,1)}, u32[]{:S(2)}, u32[]{:S(2)}) collective-permute-start(bf16[1280,2560]{1,0:T(8,128)(2,1)} %collective-permute-done.31.refs_8_), channel_id=1, source_target_pairs={{0,1},{1,0},{2,3},{3,2},{4,5},{5,4},{6,7},{7,6}} | collective-permute-start | bytes 19660808 | tf_op jit(solution)/shard_map/ppermute | solution.py:320
  1222.5 122.1 %collective-permute-start.42 = (bf16[1024,2560]{1,0:T(8,128)(2,1)}, bf16[1024,2560]{1,0:T(8,128)(2,1)}, u32[]{:S(2)}, u32[]{:S(2)}) collective-permute-start(bf16[1024,2560]{1,0:T(8,128)(2,1)} %get-tuple-element.162.h_ref), channel_id=1, source_target_pairs={{0,2},{1,3},{2,0},{3,1},{4,6},{5,7},{6,4},{7,5}} | collective-permute-start | bytes 15728648 | tf_op jit(solution)/shard_map/ppermute | solution.py:320
  1256.8 281.3 %collective-permute-start.23 = (bf16[1024,2560]{1,0:T(8,128)(2,1)}, bf16[1024,2560]{1,0:T(8,128)(2,1)}, u32[]{:S(2)}, u32[]{:S(2)}) collective-permute-start(bf16[1024,2560]{1,0:T(8,128)(2,1)} %get-tuple-element.120.h_ref), channel_id=1, source_target_pairs={{0,2},{1,3},{2,0},{3,1},{4,6},{5,7},{6,4},{7,5}} | collective-permute-start | bytes 15728648 | tf_op jit(solution)/shard_map/ppermute | solution.py:320
  1510.2 310.8 %collective-permute-start.43 = (bf16[512,2560]{1,0:T(8,128)(2,1)}, bf16[512,2560]{1,0:T(8,128)(2,1)}, u32[]{:S(2)}, u32[]{:S(2)}) collective-permute-start(bf16[512,2560]{1,0:T(8,128)(2,1)} %shard_map.144), channel_id=1, source_target_pairs={{0,2},{1,3},{2,0},{3,1},{4,6},{5,7},{6,4},{7,5}} | collective-permute-start | bytes 7864328 | tf_op jit(solution)/shard_map/ppermute | solution.py:320
  1537.6 292.1 %collective-permute-start.45 = (bf16[512,2560]{1,0:T(8,128)(2,1)}, bf16[512,2560]{1,0:T(8,128)(2,1)}, u32[]{:S(2)}, u32[]{:S(2)}) collective-permute-start(bf16[512,2560]{1,0:T(8,128)(2,1)} %shard_map.147), channel_id=1, source_target_pairs={{0,2},{1,3},{2,0},{3,1},{4,6},{5,7},{6,4},{7,5}} | collective-permute-start | bytes 7864328 | tf_op jit(solution)/shard_map/ppermute | solution.py:320
  1722.1 114.5 %collective-permute-start.33 = (bf16[1024,2560]{1,0:T(8,128)(2,1)}, bf16[1024,2560]{1,0:T(8,128)(2,1)}, u32[]{:S(2)}, u32[]{:S(2)}) collective-permute-start(bf16[1024,2560]{1,0:T(8,128)(2,1)} %shard_map.121), channel_id=1, source_target_pairs={{0,2},{1,3},{2,0},{3,1},{4,6},{5,7},{6,4},{7,5}} | collective-permute-start | bytes 15728648 | tf_op jit(solution)/shard_map/ppermute | solution.py:320
  1849.1 4.3 copy-start
  1853.4 6.6 collective-permute-start.34
  1853.6 118.1 %collective-permute-start.47 = (bf16[256,2560]{1,0:T(8,128)(2,1)S(1)}, bf16[256,2560]{1,0:T(8,128)(2,1)}, u32[]{:S(2)}, u32[]{:S(2)}) collective-permute-start(bf16[256,2560]{1,0:T(8,128)(2,1)S(1)} %get-tuple-element.202), channel_id=1, source_target_pairs={{0,5},{1,4},{2,7},{3,6},{4,1},{5,0},{6,3},{7,2}} | collective-permute-start | bytes 3932168 | tf_op jit(solution)/shard_map/ppermute | solution.py:320
  1855.5 114.8 %collective-permute-start.46 = (bf16[256,2560]{1,0:T(8,128)(2,1)S(1)}, bf16[256,2560]{1,0:T(8,128)(2,1)}, u32[]{:S(2)}, u32[]{:S(2)}) collective-permute-start(bf16[256,2560]{1,0:T(8,128)(2,1)S(1)} %get-tuple-element.203), channel_id=1, source_target_pairs={{0,4},{1,5},{2,6},{3,7},{4,0},{5,1},{6,2},{7,3}} | collective-permute-start | bytes 3932168 | tf_op jit(solution)/shard_map/ppermute | solution.py:320
  1855.7 113.1 %collective-permute-start.44 = (bf16[256,2560]{1,0:T(8,128)(2,1)S(1)}, bf16[256,2560]{1,0:T(8,128)(2,1)}, u32[]{:S(2)}, u32[]{:S(2)}) collective-permute-start(bf16[256,2560]{1,0:T(8,128)(2,1)S(1)} %slice.159), channel_id=1, source_target_pairs={{0,1},{1,0},{2,3},{3,2},{4,5},{5,4},{6,7},{7,6}} | collective-permute-start | bytes 3932168 | tf_op jit(solution)/shard_map/ppermute | solution.py:320
  1855.7 85.9 %collective-permute-start.35 = (bf16[256,2560]{1,0:T(8,128)(2,1)}, bf16[256,2560]{1,0:T(8,128)(2,1)}, u32[]{:S(2)}, u32[]{:S(2)}) collective-permute-start(bf16[256,2560]{1,0:T(8,128)(2,1)} %get-tuple-element.190), channel_id=1, source_target_pairs={{0,4},{1,5},{2,6},{3,7},{4,0},{5,1},{6,2},{7,3}} | collective-permute-start | bytes 3932168 | tf_op jit(solution)/shard_map/ppermute | solution.py:320
  1858.4 1.7 copy-start.5
  1860.1 108.4 %collective-permute-start.36 = (bf16[256,2560]{1,0:T(8,128)(2,1)S(1)}, bf16[256,2560]{1,0:T(8,128)(2,1)S(1)}, u32[]{:S(2)}, u32[]{:S(2)}) collective-permute-start(bf16[256,2560]{1,0:T(8,128)(2,1)S(1)} %copy-done.5), channel_id=1, source_target_pairs={{0,5},{1,4},{2,7},{3,6},{4,1},{5,0},{6,3},{7,2}} | collective-permute-start | bytes 3932168 | tf_op jit(solution)/shard_map/ppermute | solution.py:320
  1861.6 107.0 %copy-start.1 = (bf16[512,2560]{1,0:T(8,128)(2,1)S(1)}, bf16[512,2560]{1,0:T(8,128)(2,1)}, u32[]{:S(2)}) copy-start(bf16[512,2560]{1,0:T(8,128)(2,1)} %shard_map.145) | copy-start | bytes 7864324
  1973.2 4.1 copy-start.2
